TPU v7x, 128 devices: a whole 4x4x4 slice. The times are simulated.
128 devices in a mesh: ctx: 16 (over z, x), tp: 8 (over y, core).
Axes of the slice: x: 4, y: 4, z: 4, core: 2. Of those that a mesh axis runs over, the one named last changes fastest.
Arguments:
- hidden_in: bfloat16 [8192, 5376], P(('ctx', 'tp')), may hold values from -6 to 6
- stretch_start: int32 [1], replicated, may hold values from 1 to 1024
- pre_gain: float32 [5376], replicated, may hold values from 0.1 to 1.9
- q_weight: bfloat16 [5376, 4096], P('ctx', 'tp'), may hold values from -1 to 1
- k_weight: bfloat16 [5376, 2048], P('ctx', 'tp'), may hold values from -1 to 1
- v_weight: bfloat16 [5376, 2048], P('ctx', 'tp'), may hold values from -0.078125 to 0.078125
- o_weight: bfloat16 [4096, 5376], P('tp', 'ctx'), may hold values from -0.09375 to 0.09375
- q_gain: float32 [128], replicated, may hold values from 0.5 to 5
- k_gain: float32 [128], replicated, may hold values from 0.5 to 5
- prior_keys: bfloat16 [1024, 2048], P(None, 'tp'), may hold values from -6 to 6
- prior_values: bfloat16 [1024, 2048], P(None, 'tp'), may hold values from -6 to 6
- post_gain: float32 [5376], replicated, may hold values from 0.1 to 1.9
Outputs:
- result: bfloat16 [8192, 5376], P(('ctx', 'tp'))
All inputs are finite; a program needn't handle non-finite values.
Results may differ from a plain program's by a relative error of at most 0.013.
Values may be sent and summed in bfloat16 or wider, within the bound.
A program may use at most 128 MiB of HBM per device.

v0:
```python
import jax
import jax.numpy as jnp
from jax import lax
from jax.sharding import PartitionSpec as P

HD = 128
WINDOW = 1024
EPSILON = 1e-06
QUERY_FACTOR = 168.0 ** (-0.5)


def in_one_piece(arrays, axis, dim, along):
    ends, at = ([], 0)
    for a in arrays[:-1]:
        at += a.shape[along]
        ends.append(at)
    both = jnp.concatenate(arrays, axis=along)
    return tuple(jnp.split(lax.all_gather(both, axis, axis=dim, tiled=True), ends, axis=along))


def from_behind(value, axis, steps):
    count = lax.axis_size(axis)
    leading, last = (max(0, -steps), min(count, count - steps))
    return lax.ppermute(value, axis, [(source, source + steps) for source in range(leading, last)])


def rms_scale(inputs, scales):
    mean_sq = jnp.mean(inputs * inputs, axis=-1, keepdims=True)
    return inputs * lax.rsqrt(mean_sq + EPSILON) * scales


def rotate(inputs, positions):
    half_dim = inputs.shape[-1] // 2
    frequency = 10000.0 ** (-jnp.arange(half_dim, dtype=jnp.float32) / half_dim)
    angles = positions.astype(jnp.float32)[:, None] * frequency[None, :]
    cosines = jnp.cos(angles)[:, None, :]
    sines = jnp.sin(angles)[:, None, :]
    front = inputs[..., :half_dim]
    second = inputs[..., half_dim:]
    return jnp.concatenate(
        [front * cosines - second * sines, second * cosines + front * sines], axis=-1
    )


def local(
    hidden_in,
    stretch_start,
    pre_gain,
    q_weight,
    k_weight,
    v_weight,
    o_weight,
    q_gain,
    k_gain,
    prior_keys,
    prior_values,
    post_gain,
):
    residual_in = hidden_in.astype(jnp.float32)
    normed = rms_scale(residual_in, pre_gain).astype(jnp.bfloat16)
    block_rows = lax.all_gather(normed, "tp", axis=0, tiled=True)
    row_count = block_rows.shape[0]
    query_cols = q_weight.shape[1]
    kv_cols = k_weight.shape[1]

    def add_piece(segment):
        return jnp.dot(block_rows, segment, preferred_element_type=jnp.float32)

    segments = in_one_piece((q_weight, k_weight, v_weight), "ctx", 0, 1)
    query_raw, key_raw, value_raw = tuple((add_piece(segment) for segment in segments))
    local_heads = query_cols // HD
    local_kv = kv_cols // HD
    group = local_heads // local_kv
    chain_pos = lax.axis_index("ctx")
    positions = WINDOW + chain_pos * row_count + jnp.arange(row_count, dtype=jnp.int32)
    query = (
        rotate(rms_scale(query_raw.reshape(row_count, local_heads, HD), q_gain), positions)
        * QUERY_FACTOR
    ).astype(jnp.bfloat16)
    key_rows = (
        rotate(rms_scale(key_raw.reshape(row_count, local_kv, HD), k_gain), positions)
        .astype(jnp.bfloat16)
        .reshape(row_count, kv_cols)
    )
    value_rows = value_raw.astype(jnp.bfloat16)
    reach = WINDOW // row_count
    earlier = []
    current = (key_rows, value_rows)
    for hop_index in range(reach):
        current = from_behind((current[0], current[1]), "ctx", 1)
        earlier.append(current)
    key_parts = []
    value_parts = []
    for hop_index in range(reach - 1, -1, -1):
        source = chain_pos - (hop_index + 1)
        offset = jnp.maximum(WINDOW + source * row_count, 0)
        cached_keys = lax.dynamic_slice_in_dim(prior_keys, offset, row_count, 0)
        cached_values = lax.dynamic_slice_in_dim(prior_values, offset, row_count, 0)
        key_parts.append(jnp.where(source < 0, cached_keys, earlier[hop_index][0]))
        value_parts.append(jnp.where(source < 0, cached_values, earlier[hop_index][1]))
    key_parts.append(key_rows)
    value_parts.append(value_rows)
    span = (reach + 1) * row_count
    all_keys = jnp.concatenate(key_parts, axis=0).reshape(span, local_kv, HD)
    all_values = jnp.concatenate(value_parts, axis=0).reshape(span, local_kv, HD)
    key_anchor = WINDOW + (chain_pos - reach) * row_count
    query_grouped = query.reshape(row_count, local_kv, group, HD)
    scores = jnp.einsum(
        "qhgd,khd->hgqk", query_grouped, all_keys, preferred_element_type=jnp.float32
    )
    key_pos = key_anchor + jnp.arange(span, dtype=jnp.int32)
    first_valid = WINDOW - stretch_start[0]
    allowed = (
        (key_pos[None, :] <= positions[:, None])
        & (key_pos[None, :] > positions[:, None] - WINDOW)
        & (key_pos[None, :] >= first_valid)
    )
    scores = jnp.where(allowed[None, None, :, :], scores, jnp.float32(-1e30))
    largest = jnp.max(scores, axis=-1, keepdims=True)
    expon = jnp.exp(scores - largest)
    attn_probs = (expon / jnp.sum(expon, axis=-1, keepdims=True)).astype(jnp.bfloat16)
    attended = jnp.einsum(
        "hgqk,khd->qhgd", attn_probs, all_values, preferred_element_type=jnp.float32
    )
    attended = attended.astype(jnp.bfloat16).reshape(row_count, query_cols)
    partial_rows = jnp.dot(
        attended,
        lax.all_gather(o_weight, "ctx", axis=1, tiled=True),
        preferred_element_type=jnp.float32,
    )
    summed = lax.psum_scatter(
        partial_rows.astype(jnp.bfloat16), "tp", scatter_dimension=0, tiled=True
    ).astype(jnp.float32)
    return (residual_in + rms_scale(summed, post_gain)).astype(jnp.bfloat16)


def solution(mesh):
    return jax.shard_map(
        local,
        mesh=mesh,
        in_specs=(
            P(("ctx", "tp"), None),
            P(),
            P(),
            P("ctx", "tp"),
            P("ctx", "tp"),
            P("ctx", "tp"),
            P("tp", "ctx"),
            P(),
            P(),
            P(None, "tp"),
            P(None, "tp"),
            P(),
        ),
        out_specs=P(("ctx", "tp"), None),
        check_vma=False,
    )
```

profile of v0, /device:TPU:0, one launch (start us, length us, event | category | flops | bytes accessed | tf_op | source)
XLA Modules:
  0.0 256.0 jit_solution(17121036638809811373)
XLA Ops:
  6.5 1.3 fusion.15
  7.9 2.2 fusion.17
  10.1 0.0 all-gather.4.cloned.1.call-update
  10.1 0.0 all-gather.6.cloned.1.call-start
  10.1 2.1 pad_maximum_fusion.1
  12.3 0.0 all-gather.6.cloned.1.call-update
  12.3 0.0 all-gather.8.cloned.1.call-start
  12.3 0.7 all-gather.8.cloned.1.call-update
  13.0 0.0 reduce-scatter.2.cloned.1.call-start
  13.8 0.5 multiply_cosine_fusion
  14.3 0.1 copy.25
  14.4 0.1 copy.24
  14.6 1.9 and_and_fusion
  16.5 33.8 %all-gather.4.cloned.1.call-done = bf16[512,5376]{1,0:T(8,128)(2,1)} async-done(((bf16[64,5376]{1,0:T(8,128)(2,1)}), bf16[512,5376]{1,0:T(8,128)(2,1)}) %all-gather.4.cloned.1.call-update) | async-done | bytes 5505040 | tf_op jit(solution)/shard_map/all_gather | solution.py:61
  50.3 85.0 %all-gather.6.cloned.1.call-done = bf16[5376,1024]{1,0:T(8,128)(2,1)} async-done(((bf16[336,1024]{1,0:T(8,128)(2,1)}), bf16[5376,1024]{1,0:T(8,128)(2,1)}) %all-gather.6.cloned.1.call-update) | async-done | bytes 11010064 | tf_op jit(solution)/shard_map/all_gather | solution.py:18
  135.3 5.1 %fusion.20 = bf16[512,256]{1,0:T(8,128)(2,1)S(1)} fusion(bf16[512,5376]{1,0:T(8,128)(2,1)} %all-gather.4.cloned.1.call-done, bf16[5376,1024]{1,0:T(8,128)(2,1)} %all-gather.6.cloned.1.call-done), kind=kOutput, calls=%fused_computation.29 | convolution fusion | flops 1409417216 | bytes 8519680 | tf_op jit(solution)/shard_map/dot_general | solution.py:67
  140.4 0.0 copy-start.3
  140.4 0.0 copy-start.5
  140.4 4.2 %collective-permute-start = (bf16[512,256]{1,0:T(8,128)(2,1)S(1)}, bf16[512,256]{1,0:T(8,128)(2,1)}, u32[]{:S(2)}, u32[]{:S(2)}) collective-permute-start(bf16[512,256]{1,0:T(8,128)(2,1)S(1)} %fusion.20), channel_id=1, source_target_pairs={{0,8},{8,16},{16,24},{24,32},{32,40},{40,48},{48,56},{56,64},{64,7... | collective-permute-start | bytes 786440 | tf_op jit(solution)/shard_map/ppermute | solution.py:24
  144.6 3.5 %multiply_reduce_fusion.1 = (f32[512,2]{0,1:T(2,128)S(1)}, f32[512,256]{0,1:T(8,128)S(1)}) fusion(bf16[512,5376]{1,0:T(8,128)(2,1)S(1)} %copy-done.7, bf16[5376,1024]{1,0:T(8,128)(2,1)} %all-gather.6.cloned.1.call-done), kind=kOutput, calls=%fused_computation.43 | convolution fusion | flops 1409547264 | bytes 8785920 | tf_op jit(solution)/shard_map/dot_general | solution.py:67
  148.1 0.2 copy.23
  148.4 0.2 multiply_multiply_fusion.1
  148.6 0.2 multiply_subtract_fusion.1
  148.8 0.8 copy_bitcast_fusion
  149.7 3.5 %collective-permute-start.2 = (bf16[512,256]{1,0:T(8,128)(2,1)}, bf16[512,256]{1,0:T(8,128)(2,1)}, u32[]{:S(2)}, u32[]{:S(2)}) collective-permute-start(bf16[512,256]{1,0:T(8,128)(2,1)} %copy_bitcast_fusion), channel_id=1, source_target_pairs={{0,8},{8,16},{16,24},{24,32},{32,40},{40,48},{48,56},{56,64},{64,7... | collective-permute-start | bytes 786440 | tf_op jit(solution)/shard_map/ppermute | solution.py:24
  153.2 6.8 %multiply_reduce_fusion = (f32[512,4]{0,1:T(4,128)S(1)}, f32[512,512]{0,1:T(8,128)S(1)}) fusion(bf16[512,5376]{1,0:T(8,128)(2,1)} %all-gather.4.cloned.1.call-done, bf16[5376,1024]{1,0:T(8,128)(2,1)} %all-gather.6.cloned.1.call-done), kind=kOutput, calls=%fused_computation.33 | convolution fusion | flops 2819094528 | bytes 12066816 | tf_op jit(solution)/shard_map/dot_general | solution.py:67
  160.0 0.2 multiply_multiply_fusion
  160.2 3.1 %collective-permute-start.1 = (bf16[512,256]{1,0:T(8,128)(2,1)}, bf16[512,256]{1,0:T(8,128)(2,1)}, u32[]{:S(2)}, u32[]{:S(2)}) collective-permute-start(bf16[512,256]{1,0:T(8,128)(2,1)} %collective-permute-done), channel_id=1, source_target_pairs={{0,8},{8,16},{16,24},{24,32},{32,40},{40,48},{48,56},{56,64},{64,7... | collective-permute-start | bytes 786440 | tf_op jit(solution)/shard_map/ppermute | solution.py:24
  163.3 0.2 multiply_subtract_fusion
  163.6 0.3 copy.30
  163.9 0.3 copy.29
  164.2 0.8 maximum_convert_fusion
  165.1 3.2 %collective-permute-start.3 = (bf16[512,256]{1,0:T(8,128)(2,1)}, bf16[512,256]{1,0:T(8,128)(2,1)}, u32[]{:S(2)}, u32[]{:S(2)}) collective-permute-start(bf16[512,256]{1,0:T(8,128)(2,1)} %collective-permute-done.2), channel_id=1, source_target_pairs={{0,8},{8,16},{16,24},{24,32},{32,40},{40,48},{48,56},{56,64},{64,7... | collective-permute-start | bytes 786440 | tf_op jit(solution)/shard_map/ppermute | solution.py:24
  168.3 0.5 collective-permute-done.1
  168.7 1.2 dynamic-slice_select_fusion.1
  170.0 1.1 pad_maximum_fusion
  171.0 1.2 copy.36
  172.2 5.2 %collective-permute-done.3 = bf16[512,256]{1,0:T(8,128)(2,1)} collective-permute-done((bf16[512,256]{1,0:T(8,128)(2,1)}, bf16[512,256]{1,0:T(8,128)(2,1)}, u32[]{:S(2)}, u32[]{:S(2)}) %collective-permute-start.3) | collective-permute-done | bytes 262176 | tf_op jit(solution)/shard_map/ppermute | solution.py:24
  177.4 0.2 select_bitcast_fusion.1
  177.6 0.1 copy_bitcast_fusion.1
  177.7 10.2 %fusion.32 = (f32[2,2,512]{2,1,0:T(2,128)S(1)}, f32[2,2,512,1536]{2,3,1,0:T(8,128)}) fusion(pred[512,1536]{0,1:T(8,128)(4,1)} %and_and_fusion, bf16[512,2,128]{2,0,1:T(8,128)(2,1)} %maximum_convert_fusion, bf16[512,2,128]{2,0,1:T(8,128)(2,1)S(1)} %get-tuple-element.23, bf16[512,2,128]{2,0,1:T(8,128)(2,1)S(1)} %get-tuple-element.24, ...), kind=kOutput, calls=%fused_computation.67 | convolution fusion | flops 817890816 | bytes 15212544 | tf_op jit(solution)/shard_map/sub | solution.py:120
  187.9 5.8 %fusion.19 = bf16[2,128,2,512]{3,1,2,0:T(8,128)(2,1)S(1)} fusion(bf16[1536,2,128,1]{0,2,3,1:T(8,128)(2,1)S(1)} %bitcast.62, f32[2,2,512,1536]{2,3,1,0:T(8,128)} %get-tuple-element.20, f32[2,2,512]{2,1,0:T(2,128)S(1)} %get-tuple-element.19), kind=kOutput, calls=%fused_computation.28 | convolution fusion | flops 811859968 | bytes 13901824 | tf_op jit(solution)/shard_map/hgqk,khd->qhgd/dot_general | solution.py:122
  193.7 4.2 %all-gather.8.cloned.1.call-done = bf16[512,5376]{0,1:T(8,128)(2,1)} async-done(((bf16[512,336]{0,1:T(8,128)(2,1)}), bf16[512,5376]{0,1:T(8,128)(2,1)}) %all-gather.8.cloned.1.call-update) | async-done | bytes 5505040 | tf_op jit(solution)/shard_map/all_gather | solution.py:128
  197.9 7.5 %convolution_convert_fusion = bf16[512,5376]{1,0:T(8,128)(2,1)} fusion(bf16[512,512]{0,1:T(8,128)(2,1)S(1)} %bitcast.64, bf16[512,5376]{0,1:T(8,128)(2,1)} %all-gather.8.cloned.1.call-done), kind=kOutput, calls=%fused_computation.5 | convolution fusion | flops 2821324800 | bytes 11534336 | tf_op jit(solution)/shard_map/dot_general | solution.py:126
  205.5 0.0 reduce-scatter.2.cloned.1.call-update
  205.5 40.4 %reduce-scatter.2.cloned.1.call-done = bf16[64,5376]{1,0:T(8,128)(2,1)} async-done(((bf16[512,5376]{1,0:T(8,128)(2,1)}), bf16[64,5376]{1,0:T(8,128)(2,1)}) %reduce-scatter.2.cloned.1.call-update) | async-done | bytes 688144 | tf_op jit(solution)/shard_map/reduce_scatter | solution.py:131
  245.8 1.3 fusion.13
  247.2 2.3 fusion.18
  (26 shorter events, 0.1 us)
Async XLA Ops:
  6.5 43.8 %all-gather.4.cloned.1.call-start = ((), (), s32[]{:S(2)}) async-start(), calls=%async_computation.1 | async-start | bytes 6193152 | tf_op jit(solution)/shard_map/all_gather | solution.py:61
  10.1 125.2 %all-gather.6.cloned.1.call-start = ((), (), s32[]{:S(2)}) async-start(), calls=%async_computation.2 | async-start | bytes 11698176 | tf_op jit(solution)/shard_map/all_gather | solution.py:18
  12.3 185.7 %all-gather.8.cloned.1.call-start = ((), (), s32[]{:S(2)}) async-start(), calls=%async_computation.3 | async-start | bytes 5849088 | tf_op jit(solution)/shard_map/all_gather | solution.py:128
  13.0 232.8 %reduce-scatter.2.cloned.1.call-start = ((), (), s32[]{:S(2)}) async-start(), calls=%async_computation.4 | async-start | bytes 6193152 | tf_op jit(solution)/shard_map/reduce_scatter | solution.py:131
  135.3 9.4 %copy-start.7 = (bf16[512,5376]{1,0:T(8,128)(2,1)S(1)}, bf16[512,5376]{1,0:T(8,128)(2,1)}, u32[]{:S(2)}) copy-start(bf16[512,5376]{1,0:T(8,128)(2,1)} %all-gather.4.cloned.1.call-done) | copy-start | bytes 16515076
  140.4 7.9 %copy-start.3 = (bf16[512,256]{1,0:T(8,128)(2,1)}, bf16[512,256]{1,0:T(8,128)(2,1)S(1)}, u32[]{:S(2)}) copy-start(bf16[512,256]{1,0:T(8,128)(2,1)S(1)} %fusion.20) | copy-start | bytes 786436
  140.4 7.9 %copy-start.5 = (f32[128]{0:T(128)S(1)}, f32[128]{0:T(128)}, u32[]{:S(2)}) copy-start(f32[128]{0:T(128)} %param.20) | copy-start | bytes 1540
  140.4 19.8 %collective-permute-start = (bf16[512,256]{1,0:T(8,128)(2,1)S(1)}, bf16[512,256]{1,0:T(8,128)(2,1)}, u32[]{:S(2)}, u32[]{:S(2)}) collective-permute-start(bf16[512,256]{1,0:T(8,128)(2,1)S(1)} %fusion.20), channel_id=1, source_target_pairs={{0,8},{8,16},{16,24},{24,32},{32,40},{40,48},{48,56},{56,64},{64,7... | collective-permute-start | bytes 786440 | tf_op jit(solution)/shard_map/ppermute | solution.py:24
  149.7 10.3 %copy-start.6 = (f32[128]{0:T(128)S(1)}, f32[128]{0:T(128)}, u32[]{:S(2)}) copy-start(f32[128]{0:T(128)} %param.19) | copy-start | bytes 1540
  149.7 15.4 %collective-permute-start.2 = (bf16[512,256]{1,0:T(8,128)(2,1)}, bf16[512,256]{1,0:T(8,128)(2,1)}, u32[]{:S(2)}, u32[]{:S(2)}) collective-permute-start(bf16[512,256]{1,0:T(8,128)(2,1)} %copy_bitcast_fusion), channel_id=1, source_target_pairs={{0,8},{8,16},{16,24},{24,32},{32,40},{40,48},{48,56},{56,64},{64,7... | collective-permute-start | bytes 786440 | tf_op jit(solution)/shard_map/ppermute | solution.py:24
  160.2 8.5 %collective-permute-start.1 = (bf16[512,256]{1,0:T(8,128)(2,1)}, bf16[512,256]{1,0:T(8,128)(2,1)}, u32[]{:S(2)}, u32[]{:S(2)}) collective-permute-start(bf16[512,256]{1,0:T(8,128)(2,1)} %collective-permute-done), channel_id=1, source_target_pairs={{0,8},{8,16},{16,24},{24,32},{32,40},{40,48},{48,56},{56,64},{64,7... | collective-permute-start | bytes 786440 | tf_op jit(solution)/shard_map/ppermute | solution.py:24
  164.2 13.2 %copy-start.2 = (bf16[1024,256]{1,0:T(8,128)(2,1)S(1)}, bf16[1024,256]{1,0:T(8,128)(2,1)}, u32[]{:S(2)}) copy-start(bf16[1024,256]{1,0:T(8,128)(2,1)} %param.21) | copy-start | bytes 1572868
  165.1 12.3 %collective-permute-start.3 = (bf16[512,256]{1,0:T(8,128)(2,1)}, bf16[512,256]{1,0:T(8,128)(2,1)}, u32[]{:S(2)}, u32[]{:S(2)}) collective-permute-start(bf16[512,256]{1,0:T(8,128)(2,1)} %collective-permute-done.2), channel_id=1, source_target_pairs={{0,8},{8,16},{16,24},{24,32},{32,40},{40,48},{48,56},{56,64},{64,7... | collective-permute-start | bytes 786440 | tf_op jit(solution)/shard_map/ppermute | solution.py:24
  177.7 10.2 %copy-start.1 = (bf16[1536,256]{0,1:T(8,128)(2,1)S(1)}, bf16[1536,256]{0,1:T(8,128)(2,1)}, u32[]{:S(2)}) copy-start(bf16[1536,256]{0,1:T(8,128)(2,1)} %copy.36) | copy-start | bytes 2359300
  205.5 41.7 %copy-start = (bf16[64,5376]{1,0:T(8,128)(2,1)S(1)}, bf16[64,5376]{1,0:T(8,128)(2,1)}, u32[]{:S(2)}) copy-start(bf16[64,5376]{1,0:T(8,128)(2,1)} %param.12) | copy-start | bytes 2064388
  205.5 41.7 %copy-start.4 = (f32[5376]{0:T(1024)S(1)}, f32[5376]{0:T(1024)}, u32[]{:S(2)}) copy-start(f32[5376]{0:T(1024)} %param.23) | copy-start | bytes 64516
Sparse Core Ops, SparseCore 0:
  10.2 40.0 all-gather.3
  52.4 82.7 all-gather.5
  137.4 60.4 all-gather.7
  205.6 40.1 reduce-scatter.1
where the time goes:
time: 257 us; the launch traced here: 256 us
  waiting for transfers between devices  170 us (66%)
  matrix products  38.9 us (15%)
  other arithmetic  16.7 us (6%)
  starting transfers between devices  14.1 us (5%)
  between operations  14 us (5%)
    all_gather x1, waiting for transfers between devices, in_one_piece(): lax.all_gather(both, axis, axis=dim, tiled=True)  85 us
    reduce_scatter x1, waiting for transfers between devices, local(): lax.psum_scatter(partial_rows.astype(jnp.bfloat16), 'tp', scatter_dimensi...  40.4 us
    all_gather x1, waiting for transfers between devices, local(): block_rows = lax.all_gather(normed, 'tp', axis=0, tiled=True)  33.8 us
    dot_general x3, matrix products, add_piece(): return jnp.dot(block_rows, segment, preferred_element_type=jnp.float32)  15.4 us
    ppermute x4, starting transfers between devices, from_behind(): lax.ppermute(value, axis, [(source, source + steps) for source in range(l...  14 us
    sub x1, matrix products, local(): expon = jnp.exp(scores - largest)  10.2 us
    dot_general x1, matrix products, local(): jnp.dot(attended, lax.all_gather(o_weight, 'ctx', axis=1, tiled=True), pr...  7.51 us
    dot_general x1, matrix products, local(): jnp.einsum('hgqk,khd->qhgd', attn_probs, all_values, preferred_element_ty...  5.77 us
  transfers between devices with their start and end apart: 8, of which 6 were waited for; matrix products, arithmetic and copies ran while one was open for 17% of the time, Pallas kernels for 0%

commit v1 on v0

--- a/solution.py
+++ b/solution.py
@@ -58,7 +58,10 @@
 ):
     residual_in = hidden_in.astype(jnp.float32)
     normed = rms_scale(residual_in, pre_gain).astype(jnp.bfloat16)
-    block_rows = lax.all_gather(normed, "tp", axis=0, tiled=True)
+    size = lax.axis_size("tp")
+    parts = jnp.stack([normed for _ in range(size)])
+    parts = lax.all_to_all(parts, "tp", split_axis=0, concat_axis=0)
+    block_rows = jnp.concatenate(parts, axis=0)
     row_count = block_rows.shape[0]
     query_cols = q_weight.shape[1]
     kv_cols = k_weight.shape[1]

time: 257 us -> 248 us (0.965)
  waiting for transfers between devices: 170 us -> 134 us
  local copies, waits for them, and re-layouts: 2.41 us -> 24.8 us
  starting transfers between devices: 14.1 us -> 18.5 us
    all_gather x1 -> x0, waiting for transfers between devices: 33.8 us -> none  [local(): block_rows = lax.all_gather(normed, 'tp', axis=0, tiled=True)]
    dot_general x0 -> x4, local copies, waits for them, and re-layouts: none -> 18.3 us  [add_piece(): return jnp.dot(block_rows, segment, preferred_element_type=jnp.float32)]
    all_gather x1, waiting for transfers between devices: 85 us -> 72 us  [in_one_piece(): lax.all_gather(both, axis, axis=dim, tiled=True)]
    ppermute x4, waiting for transfers between devices: 5.67 us -> 18.5 us  [from_behind(): lax.ppermute(value, axis, [(source, source + steps) for source in range(l...]
    all_to_all x0 -> x1, starting transfers between devices: none -> 4.67 us  [local(): parts = lax.all_to_all(parts, 'tp', split_axis=0, concat_axis=0)]
    all_gather x1, waiting for transfers between devices: 4.23 us -> 0.02 us  [local(): lax.all_gather(o_weight, 'ctx', axis=1, tiled=True)]
    another operation x0 -> x1, local copies, waits for them, and re-layouts: none -> 2.83 us  [local(): parts = jnp.stack([normed for _ in range(size)])]
  transfers between devices with their start and end apart: 8 -> 8, of which waited for: 6 -> 4; matrix products, arithmetic and copies ran while one was open for 17% -> 27% of each run, Pallas kernels for 0% -> 0%
where the time goes in v1:
time: 248 us; the launch traced here: 247 us
  waiting for transfers between devices  134 us (54%)
  matrix products  40.5 us (16%)
  local copies, waits for them, and re-layouts  24.8 us (10%)
  starting transfers between devices  18.5 us (7%)
  other arithmetic  14.8 us (6%)
  between operations  14 us (6%)
    all_gather x1, waiting for transfers between devices, in_one_piece(): lax.all_gather(both, axis, axis=dim, tiled=True)  72 us
    reduce_scatter x1, waiting for transfers between devices, local(): lax.psum_scatter(partial_rows.astype(jnp.bfloat16), 'tp', scatter_dimensi...  42.8 us
    ppermute x4, waiting for transfers between devices, from_behind(): lax.ppermute(value, axis, [(source, source + steps) for source in range(l...  18.5 us
    dot_general x4, local copies, waits for them, and re-layouts, add_piece(): return jnp.dot(block_rows, segment, preferred_element_type=jnp.float32)  18.3 us
    dot_general x3, matrix products, add_piece(): return jnp.dot(block_rows, segment, preferred_element_type=jnp.float32)  16.7 us
    ppermute x4, starting transfers between devices, from_behind(): lax.ppermute(value, axis, [(source, source + steps) for source in range(l...  13.8 us
    sub x1, matrix products, local(): expon = jnp.exp(scores - largest)  10.7 us
    dot_general x1, matrix products, local(): jnp.dot(attended, lax.all_gather(o_weight, 'ctx', axis=1, tiled=True), pr...  7.55 us
  transfers between devices with their start and end apart: 8, of which 4 were waited for; matrix products, arithmetic and copies ran while one was open for 27% of the time, Pallas kernels for 0%

profile of v1, /device:TPU:0, one launch (start us, length us, event | category | flops | bytes accessed | tf_op | source)
XLA Modules:
  0.0 246.7 jit_solution(16467699194326733964)
XLA Ops:
  6.5 2.1 pad_maximum_fusion.1
  8.6 0.0 all-gather.3.cloned.1.call-update
  8.7 1.3 fusion.11
  10.0 1.3 fusion.13
  11.3 2.8 %stack.2 = bf16[8,64,5376]{2,1,0:T(8,128)(2,1)} broadcast(bf16[64,5376]{1,0:T(8,128)(2,1)S(1)} %fusion.13), dimensions={1,2} | broadcast | bytes 6193152 | tf_op jit(solution)/shard_map/stack | solution.py:62
  14.2 4.7 %all-to-all-start = ((bf16[8,64,5376]{2,1,0:T(8,128)(2,1)}), bf16[8,64,5376]{2,1,0:T(8,128)(2,1)}, u32[]{:S(2)}, u32[]{:S(2)}) async-start(bf16[8,64,5376]{2,1,0:T(8,128)(2,1)} %stack.2), calls=%async_computation | async-start | bytes 11010048 | tf_op jit(solution)/shard_map/all_to_all | solution.py:63
  18.8 0.0 all-gather.5.cloned.1.call-start
  18.9 0.7 all-gather.5.cloned.1.call-update
  19.6 0.0 reduce-scatter.2.cloned.1.call-start
  20.4 0.5 multiply_cosine_fusion
  20.9 1.9 and_and_fusion
  22.8 72.0 %all-gather.3.cloned.1.call-done = bf16[5376,1024]{1,0:T(8,128)(2,1)} async-done(((bf16[336,1024]{1,0:T(8,128)(2,1)}), bf16[5376,1024]{1,0:T(8,128)(2,1)}) %all-gather.3.cloned.1.call-update) | async-done | bytes 11010064 | tf_op jit(solution)/shard_map/all_gather | solution.py:18
  94.8 2.0 slice_bitcast_fusion.1
  96.7 3.0 %copy.13 = bf16[256,5376]{1,0:T(8,128)(2,1)} copy(bf16[256,5376]{0,1:T(8,128)(2,1)S(1)} %slice_bitcast_fusion.1) | data formatting | bytes 5505024 | tf_op jit(solution)/shard_map/dot_general | solution.py:70
  99.7 0.0 all-to-all-done
  99.7 5.0 %multiply_reduce_fusion.1 = (f32[512,2]{0,1:T(2,128)S(1)}, f32[512,2,128]{0,2,1:T(8,128)S(1)}) fusion(bf16[512,5376,1]{1,0,2:T(8,128)(2,1)} %bitcast.5, bf16[2,128,5376]{2,1,0:T(8,128)(2,1)} %bitcast.57), kind=kOutput, calls=%fused_computation.39 | convolution fusion | flops 1409547264 | bytes 8785920 | tf_op jit(solution)/shard_map/dot_general | solution.py:70
  104.8 0.1 multiply_multiply_fusion.1
  104.9 0.1 multiply_subtract_fusion.1
  105.1 0.1 copy.27
  105.2 4.1 %collective-permute-start.2 = (bf16[512,256]{1,0:T(8,128)(2,1)S(1)}, bf16[512,256]{1,0:T(8,128)(2,1)}, u32[]{:S(2)}, u32[]{:S(2)}) collective-permute-start(bf16[512,256]{1,0:T(8,128)(2,1)S(1)} %copy.27), channel_id=1, source_target_pairs={{0,8},{8,16},{16,24},{24,32},{32,40},{40,48},{48,56},{56,64},{64,7... | collective-permute-start | bytes 786440 | tf_op jit(solution)/shard_map/ppermute | solution.py:24
  109.3 5.0 %fusion.16 = bf16[512,256]{1,0:T(8,128)(2,1)S(1)} fusion(bf16[512,5376]{1,0:T(8,128)(2,1)} %bitcast, bf16[5376,1024]{1,0:T(8,128)(2,1)} %all-gather.3.cloned.1.call-done), kind=kOutput, calls=%fused_computation.27 | convolution fusion | flops 1409417216 | bytes 8519680 | tf_op jit(solution)/shard_map/dot_general | solution.py:70
  114.3 0.0 copy-start.2
  114.3 3.4 %collective-permute-start = (bf16[512,256]{1,0:T(8,128)(2,1)S(1)}, bf16[512,256]{1,0:T(8,128)(2,1)}, u32[]{:S(2)}, u32[]{:S(2)}) collective-permute-start(bf16[512,256]{1,0:T(8,128)(2,1)S(1)} %fusion.16), channel_id=1, source_target_pairs={{0,8},{8,16},{16,24},{24,32},{32,40},{40,48},{48,56},{56,64},{64,7... | collective-permute-start | bytes 786440 | tf_op jit(solution)/shard_map/ppermute | solution.py:24
  117.7 5.4 %slice_bitcast_fusion = bf16[512,5376]{0,1:T(8,128)(2,1)} fusion(bf16[5376,1024]{1,0:T(8,128)(2,1)} %all-gather.3.cloned.1.call-done), kind=kLoop, calls=%fused_computation.10 | loop fusion | bytes 11010048 | tf_op jit(solution)/shard_map/dot_general | solution.py:70
  123.0 8.0 %copy.17 = bf16[512,5376]{1,0:T(8,128)(2,1)} copy(bf16[512,5376]{0,1:T(8,128)(2,1)} %slice_bitcast_fusion) | data formatting | bytes 11010048 | tf_op jit(solution)/shard_map/dot_general | solution.py:70
  131.1 6.7 %multiply_reduce_fusion = (f32[512,4]{0,1:T(4,128)S(1)}, f32[512,4,128]{0,2,1:T(8,128)S(1)}) fusion(bf16[512,5376,1]{1,0,2:T(8,128)(2,1)} %bitcast.5, bf16[4,128,5376]{2,1,0:T(8,128)(2,1)} %bitcast.56), kind=kOutput, calls=%fused_computation.31 | convolution fusion | flops 2819094528 | bytes 12066816 | tf_op jit(solution)/shard_map/dot_general | solution.py:70
  137.8 0.2 multiply_multiply_fusion
  138.0 0.0 collective-permute-done.2
  138.0 3.1 %collective-permute-start.3 = (bf16[512,256]{1,0:T(8,128)(2,1)}, bf16[512,256]{1,0:T(8,128)(2,1)}, u32[]{:S(2)}, u32[]{:S(2)}) collective-permute-start(bf16[512,256]{1,0:T(8,128)(2,1)} %collective-permute-done.2), channel_id=1, source_target_pairs={{0,8},{8,16},{16,24},{24,32},{32,40},{40,48},{48,56},{56,64},{64,7... | collective-permute-start | bytes 786440 | tf_op jit(solution)/shard_map/ppermute | solution.py:24
  141.1 3.2 %collective-permute-start.1 = (bf16[512,256]{1,0:T(8,128)(2,1)}, bf16[512,256]{1,0:T(8,128)(2,1)}, u32[]{:S(2)}, u32[]{:S(2)}) collective-permute-start(bf16[512,256]{1,0:T(8,128)(2,1)} %collective-permute-done), channel_id=1, source_target_pairs={{0,8},{8,16},{16,24},{24,32},{32,40},{40,48},{48,56},{56,64},{64,7... | collective-permute-start | bytes 786440 | tf_op jit(solution)/shard_map/ppermute | solution.py:24
  144.3 0.2 multiply_subtract_fusion
  144.5 0.3 copy.18
  144.9 0.3 copy.19
  145.2 7.8 %collective-permute-done.3 = bf16[512,256]{1,0:T(8,128)(2,1)} collective-permute-done((bf16[512,256]{1,0:T(8,128)(2,1)}, bf16[512,256]{1,0:T(8,128)(2,1)}, u32[]{:S(2)}, u32[]{:S(2)}) %collective-permute-start.3) | collective-permute-done | bytes 262176 | tf_op jit(solution)/shard_map/ppermute | solution.py:24
  153.0 10.7 %collective-permute-done.1 = bf16[512,256]{1,0:T(8,128)(2,1)} collective-permute-done((bf16[512,256]{1,0:T(8,128)(2,1)}, bf16[512,256]{1,0:T(8,128)(2,1)}, u32[]{:S(2)}, u32[]{:S(2)}) %collective-permute-start.1) | collective-permute-done | bytes 262176 | tf_op jit(solution)/shard_map/ppermute | solution.py:24
  163.7 2.3 dynamic-slice_select_fusion.1
  165.9 0.8 copy.29
  166.8 0.8 copy.28
  167.6 1.1 pad_maximum_fusion
  168.7 1.2 copy.26
  169.9 10.7 %fusion.28 = (f32[2,2,512]{2,1,0:T(2,128)S(1)}, f32[2,2,512,1536]{2,3,1,0:T(8,128)}) fusion(pred[512,1536]{0,1:T(8,128)(4,1)} %and_and_fusion, bf16[512,2,128]{0,2,1:T(8,128)(2,1)S(1)} %maximum_convert_fusion, bf16[512,2,128]{0,2,1:T(8,128)(2,1)} %bitcast.62, bf16[512,2,128]{0,2,1:T(8,128)(2,1)} %bitcast.63, f32[512,2,2,64]{3,0,2,1:T(8,128)S(1)} %copy.19, ...), kind=kOutput, calls=%fused_computation.62 | convolution fusion | flops 817890816 | bytes 15212544 | tf_op jit(solution)/shard_map/sub | solution.py:123
  180.6 5.6 %fusion.15 = bf16[2,128,2,512]{3,1,2,0:T(8,128)(2,1)S(1)} fusion(bf16[1536,2,128,1]{0,2,3,1:T(8,128)(2,1)S(1)} %bitcast.61, f32[2,2,512,1536]{2,3,1,0:T(8,128)} %get-tuple-element.20, f32[2,2,512]{2,1,0:T(2,128)S(1)} %get-tuple-element.19), kind=kOutput, calls=%fused_computation.26 | convolution fusion | flops 811859968 | bytes 13901824 | tf_op jit(solution)/shard_map/hgqk,khd->qhgd/dot_general | solution.py:125
  186.1 0.0 all-gather.5.cloned.1.call-done
  186.2 7.5 %convolution_convert_fusion = bf16[512,5376]{1,0:T(8,128)(2,1)} fusion(bf16[512,512]{0,1:T(8,128)(2,1)S(1)} %bitcast.64, bf16[512,5376]{0,1:T(8,128)(2,1)} %all-gather.5.cloned.1.call-done), kind=kOutput, calls=%fused_computation.5 | convolution fusion | flops 2821324800 | bytes 11534336 | tf_op jit(solution)/shard_map/dot_general | solution.py:129
  193.7 0.0 reduce-scatter.2.cloned.1.call-update
  193.7 42.8 %reduce-scatter.2.cloned.1.call-done = bf16[64,5376]{1,0:T(8,128)(2,1)} async-done(((bf16[512,5376]{1,0:T(8,128)(2,1)}), bf16[64,5376]{1,0:T(8,128)(2,1)}) %reduce-scatter.2.cloned.1.call-update) | async-done | bytes 688144 | tf_op jit(solution)/shard_map/reduce_scatter | solution.py:134
  236.5 1.3 fusion.9
  237.9 2.3 fusion.14
  (23 shorter events, 0.1 us)
Async XLA Ops:
  6.5 88.2 %all-gather.3.cloned.1.call-start = ((), (), s32[]{:S(2)}) async-start(), calls=%async_computation.2 | async-start | bytes 11698176 | tf_op jit(solution)/shard_map/all_gather | solution.py:18
  14.2 85.6 %all-to-all-start = ((bf16[8,64,5376]{2,1,0:T(8,128)(2,1)}), bf16[8,64,5376]{2,1,0:T(8,128)(2,1)}, u32[]{:S(2)}, u32[]{:S(2)}) async-start(bf16[8,64,5376]{2,1,0:T(8,128)(2,1)} %stack.2), calls=%async_computation | async-start | bytes 11010048 | tf_op jit(solution)/shard_map/all_to_all | solution.py:63
  18.8 167.3 %all-gather.5.cloned.1.call-start = ((), (), s32[]{:S(2)}) async-start(), calls=%async_computation.3 | async-start | bytes 5849088 | tf_op jit(solution)/shard_map/all_gather | solution.py:131
  19.6 216.9 %reduce-scatter.2.cloned.1.call-start = ((), (), s32[]{:S(2)}) async-start(), calls=%async_computation.4 | async-start | bytes 6193152 | tf_op jit(solution)/shard_map/reduce_scatter | solution.py:134
  99.7 5.1 %copy-start.4 = (f32[128]{0:T(128)S(1)}, f32[128]{0:T(128)}, u32[]{:S(2)}) copy-start(f32[128]{0:T(128)} %param.20) | copy-start | bytes 1540
  105.2 32.8 %collective-permute-start.2 = (bf16[512,256]{1,0:T(8,128)(2,1)S(1)}, bf16[512,256]{1,0:T(8,128)(2,1)}, u32[]{:S(2)}, u32[]{:S(2)}) collective-permute-start(bf16[512,256]{1,0:T(8,128)(2,1)S(1)} %copy.27), channel_id=1, source_target_pairs={{0,8},{8,16},{16,24},{24,32},{32,40},{40,48},{48,56},{56,64},{64,7... | collective-permute-start | bytes 786440 | tf_op jit(solution)/shard_map/ppermute | solution.py:24
  114.3 16.8 %copy-start.2 = (bf16[512,256]{1,0:T(8,128)(2,1)}, bf16[512,256]{1,0:T(8,128)(2,1)S(1)}, u32[]{:S(2)}) copy-start(bf16[512,256]{1,0:T(8,128)(2,1)S(1)} %fusion.16) | copy-start | bytes 786436
  114.3 26.8 %collective-permute-start = (bf16[512,256]{1,0:T(8,128)(2,1)S(1)}, bf16[512,256]{1,0:T(8,128)(2,1)}, u32[]{:S(2)}, u32[]{:S(2)}) collective-permute-start(bf16[512,256]{1,0:T(8,128)(2,1)S(1)} %fusion.16), channel_id=1, source_target_pairs={{0,8},{8,16},{16,24},{24,32},{32,40},{40,48},{48,56},{56,64},{64,7... | collective-permute-start | bytes 786440 | tf_op jit(solution)/shard_map/ppermute | solution.py:24
  131.1 6.7 %copy-start.5 = (f32[128]{0:T(128)S(1)}, f32[128]{0:T(128)}, u32[]{:S(2)}) copy-start(f32[128]{0:T(128)} %param.19) | copy-start | bytes 1540
  138.0 15.0 %collective-permute-start.3 = (bf16[512,256]{1,0:T(8,128)(2,1)}, bf16[512,256]{1,0:T(8,128)(2,1)}, u32[]{:S(2)}, u32[]{:S(2)}) collective-permute-start(bf16[512,256]{1,0:T(8,128)(2,1)} %collective-permute-done.2), channel_id=1, source_target_pairs={{0,8},{8,16},{16,24},{24,32},{32,40},{40,48},{48,56},{56,64},{64,7... | collective-permute-start | bytes 786440 | tf_op jit(solution)/shard_map/ppermute | solution.py:24
  141.1 22.6 %collective-permute-start.1 = (bf16[512,256]{1,0:T(8,128)(2,1)}, bf16[512,256]{1,0:T(8,128)(2,1)}, u32[]{:S(2)}, u32[]{:S(2)}) collective-permute-start(bf16[512,256]{1,0:T(8,128)(2,1)} %collective-permute-done), channel_id=1, source_target_pairs={{0,8},{8,16},{16,24},{24,32},{32,40},{40,48},{48,56},{56,64},{64,7... | collective-permute-start | bytes 786440 | tf_op jit(solution)/shard_map/ppermute | solution.py:24
  169.9 10.7 %copy-start.1 = (bf16[1536,256]{0,1:T(8,128)(2,1)S(1)}, bf16[1536,256]{0,1:T(8,128)(2,1)}, u32[]{:S(2)}) copy-start(bf16[1536,256]{0,1:T(8,128)(2,1)} %copy.26) | copy-start | bytes 2359300
  193.7 44.1 %copy-start = (bf16[64,5376]{1,0:T(8,128)(2,1)S(1)}, bf16[64,5376]{1,0:T(8,128)(2,1)}, u32[]{:S(2)}) copy-start(bf16[64,5376]{1,0:T(8,128)(2,1)} %param.12) | copy-start | bytes 2064388
  193.7 44.2 %copy-start.3 = (f32[5376]{0:T(1024)S(1)}, f32[5376]{0:T(1024)}, u32[]{:S(2)}) copy-start(f32[5376]{0:T(1024)} %param.23) | copy-start | bytes 64516
Sparse Core Ops, SparseCore 0:
  9.5 85.2 all-gather.2
  96.9 74.3 all-gather.4
  193.9 42.6 reduce-scatter.1
